TPU v7x, 32 devices: a whole 2x2x4 slice. The times are simulated.
32 devices in a mesh: seg: 4 (over z), cp: 8 (over y, x, core).
Axes of the slice: x: 2, y: 2, z: 4, core: 2. Of those that a mesh axis runs over, the one named last changes fastest.
Arguments:
- mixed_qkv: bfloat16 [4096, 8192], P(('seg', 'cp')), may hold values from -6 to 6
- gate_z: bfloat16 [4096, 4096], P(('seg', 'cp')), may hold values from -6 to 6
- gate_logits: bfloat16 [4096, 64], P(('seg', 'cp')), may hold values from -16 to 4
- block_table: int32 [4, 16], P('seg'), may hold values from 0 to 15, as said below
- conv_weight: float32 [4, 8192], replicated, may hold values from -3 to 3
- a_log: float32 [32], replicated, may hold values from -0.7 to 0.7
- dt_bias: float32 [32], replicated, may hold values from -0.5 to 0.5
- norm_gain: float32 [128], replicated, may hold values from 0.25 to 1.75
Outputs:
- mixed_out: bfloat16 [4096, 4096], P(('seg', 'cp'))
Inputs may be any that keep to these rules, and one draw needn't show every extreme that they name: Each row of block_table is a permutation of the numbers 0 to 15; its entries at even positions are below 8, those at odd positions are 8 or more.
All inputs are finite; a program needn't handle non-finite values.
Results may differ from a plain program's by a relative error of at most 0.001.
Values may be sent and summed in bfloat16 or wider, within the bound.
A program may use at most 128 MiB of HBM per device.

v0:
```python
import functools

import jax
import jax.numpy as jnp
from jax import lax
from jax.experimental import pallas as pl
from jax.experimental.pallas import tpu as pltpu
from jax.sharding import PartitionSpec as P

VALUE_HEADS = 32
KEY_HEADS = 16
HEAD_DIM = 128
CONV = 4
BLOCK = 128
TAIL = 16
GROUP = VALUE_HEADS // KEY_HEADS

f32 = jnp.float32
bf16 = jnp.bfloat16
MESH = pl.DeviceIdType.MESH
highest = lax.Precision.HIGHEST


def split(x):
    hi = x.astype(bf16)
    return hi, (x - hi.astype(f32)).astype(bf16)


NN = (((1,), (0,)), ((), ()))
NT = (((1,), (1,)), ((), ()))


def mm(a, b, dims=NN):
    def dot(x, y):
        return lax.dot_general(x, y, dims, preferred_element_type=f32)

    return dot(a[0], b[0]) + (dot(a[0], b[1]) + dot(a[1], b[0]))


def scatter_kernel(n, segs, heads, qkv, z, gates, oq, ok, ov, oz, og, otail, send, recv, local):
    me = lax.axis_index("cp")
    seg = lax.axis_index("seg")
    after = lax.rem(seg + 1, segs)
    before = lax.rem(seg + segs - 1, segs)
    keys = max(1, heads // GROUP)
    wk, wv = keys * HEAD_DIM, heads * HEAD_DIM
    key_width = KEY_HEADS * HEAD_DIM
    rows = qkv.shape[0]

    barrier = pltpu.get_barrier_semaphore()
    for d in range(n):
        peer = lax.rem(me + d, n)
        if d:
            pl.semaphore_signal(barrier, inc=1, device_id=(seg, peer), device_id_type=MESH)
        pl.semaphore_signal(barrier, inc=1, device_id=(before, peer), device_id_type=MESH)
    pl.semaphore_wait(barrier, 2 * n - 1)

    def columns(start, width):
        return pl.ds(pl.multiple_of(start, HEAD_DIM), width)

    def pieces(p, slot):
        kcol = lax.div(p * heads, GROUP) * HEAD_DIM
        vcol = p * wv
        return [
            (qkv.at[:, columns(kcol, wk)], oq.at[slot]),
            (qkv.at[:, columns(key_width + kcol, wk)], ok.at[slot]),
            (qkv.at[:, columns(2 * key_width + vcol, wv)], ov.at[slot]),
            (gates, og.at[slot]),
            (z.at[:, columns(vcol, wv)], oz.at[slot]),
        ]

    def tails(p, slot):
        kcol = lax.div(p * heads, GROUP) * HEAD_DIM
        vcol = p * wv
        last = pl.ds(rows - TAIL, TAIL)
        return [
            (qkv.at[last, columns(kcol, wk)], otail.at[slot, :, pl.ds(0, wk)]),
            (qkv.at[last, columns(key_width + kcol, wk)], otail.at[slot, :, pl.ds(wk, wk)]),
            (qkv.at[last, columns(2 * key_width + vcol, wv)], otail.at[slot, :, pl.ds(2 * wk, wv)]),
        ]

    started = []

    def post(kind, src, dst, peer, target):
        copy = pltpu.make_async_remote_copy(
            src_ref=src,
            dst_ref=dst,
            send_sem=send.at[kind, peer],
            recv_sem=recv.at[kind, me],
            device_id=target,
            device_id_type=MESH,
        )
        copy.start()
        started.append(copy)

    order = sorted(range(1, n), key=lambda d: -min(d, n - d))
    for kinds in ((0, 1, 2, 3), (4,)):
        for d in order:
            peer = lax.rem(me + d, n)
            for kind in kinds:
                src, dst = pieces(peer, me)[kind]
                post(kind, src, dst, peer, (seg, peer))
        if kinds[0] == 0:
            for d in range(n):
                peer = lax.rem(me + d, n)
                for i, (src, dst) in enumerate(tails(peer, me)):
                    post(5 + i, src, dst, peer, (after, peer))
    own = []
    for kind, (src, dst) in enumerate(pieces(me, me)):
        copy = pltpu.make_async_copy(src, dst, local.at[kind])
        copy.start()
        own.append(copy)
    for copy in own:
        copy.wait()
    for d in range(n):
        source = lax.rem(me + n - d, n)
        found = list(enumerate(pieces(me, source))) if d else []
        found += [(5 + i, pair) for i, pair in enumerate(tails(me, source))]
        for kind, (src, dst) in found:
            pltpu.make_async_remote_copy(
                src_ref=src,
                dst_ref=dst,
                send_sem=send.at[kind, source],
                recv_sem=recv.at[kind, source],
                device_id=(seg, source),
                device_id_type=MESH,
            ).wait_recv()
    for copy in started:
        copy.wait_send()


def scatter(n, segs, heads, qkv, z, gates):
    keys = max(1, heads // GROUP)
    wk, wv = keys * HEAD_DIM, heads * HEAD_DIM
    rows = qkv.shape[0]

    def shape(*dims):
        return jax.ShapeDtypeStruct(dims, bf16)

    return pl.pallas_call(
        functools.partial(scatter_kernel, n, segs, heads),
        out_shape=(
            shape(n, rows, wk),
            shape(n, rows, wk),
            shape(n, rows, wv),
            shape(n, rows, wv),
            shape(n, rows, gates.shape[1]),
            shape(n, TAIL, 2 * wk + wv),
        ),
        in_specs=[pl.BlockSpec(memory_space=pl.ANY)] * 3,
        out_specs=[pl.BlockSpec(memory_space=pltpu.VMEM)] * 6,
        scratch_shapes=[
            pltpu.SemaphoreType.DMA((8, n)),
            pltpu.SemaphoreType.DMA((8, n)),
            pltpu.SemaphoreType.DMA((5,)),
        ],
        compiler_params=pltpu.CompilerParams(collective_id=0, has_side_effects=True),
        name="scatter",
    )(qkv, z, gates)


def log1p_exact(y):
    u = 1.0 + y
    return jnp.where(u == 1.0, y, jnp.log(u) * (y / jnp.where(u == 1.0, 1.0, u - 1.0)))


def local_kernel(
    heads, meta, q_ref, k_ref, v_ref, g_ref, tail_ref, w_ref, rate_ref, o_ref, m_ref, end_ref, x_ref, st_ref
):
    keys = max(1, heads // GROUP)
    wk, wv = keys * HEAD_DIM, heads * HEAD_DIM
    total = 2 * pl.num_programs(0)
    b = pl.program_id(0)
    i0 = meta[2 * b]
    i1 = meta[2 * b + 1]
    ip = meta[jnp.maximum(2 * b - 1, 0)]
    tail_from = meta[total]
    no_tail = meta[total + 1]
    head_start = meta[total + 2]
    half = q_ref.shape[1]

    row = lax.broadcasted_iota(jnp.int32, (BLOCK, BLOCK), 0)
    col = lax.broadcasted_iota(jnp.int32, (BLOCK, BLOCK), 1)
    strict = row > col
    inclusive = row >= col
    eye = jnp.where(row == col, 1.0, 0.0).astype(f32)

    @pl.when(b == 0)
    def _():
        for h in range(heads):
            st_ref[h, :, :HEAD_DIM] = jnp.zeros((HEAD_DIM, HEAD_DIM), f32)
            st_ref[h, :, HEAD_DIM:] = eye

    tail_rows = jnp.where(no_tail > 0, 0.0, tail_ref[tail_from].astype(f32))[TAIL - 8 :]
    at = 0
    for ref, width in ((q_ref, wk), (k_ref, wk), (v_ref, wv)):
        cols = slice(at, at + width)
        prior = ref[ip, half - 16 :, :].astype(f32)[8:]
        x_ref[0:8, cols] = jnp.where(b == 0, tail_rows[:, cols], prior)
        x_ref[8 : 8 + half, cols] = ref[i0].astype(f32)
        x_ref[8 + half : 8 + 2 * half, cols] = ref[i1].astype(f32)
        at += width

    def conv(start):
        cols = slice(start, start + HEAD_DIM)
        total_rows = w_ref[0:1, cols] * x_ref[5 : 5 + BLOCK, cols]
        for j in range(1, CONV):
            total_rows = total_rows + w_ref[j : j + 1, cols] * x_ref[5 + j : 5 + j + BLOCK, cols]
        return total_rows / (1.0 + jnp.exp(-total_rows))

    def unit(x):
        return x * lax.rsqrt(jnp.sum(x * x, axis=-1, keepdims=True) + 1e-06)

    gates = jnp.concatenate([g_ref[i0], g_ref[i1]], axis=0).astype(f32)
    gates = jnp.concatenate([gates, jnp.zeros((BLOCK, BLOCK - gates.shape[1]), f32)], axis=1)
    beta_all = 1.0 / (1.0 + jnp.exp(-gates))
    shifted = gates + rate_ref[1:2, :]
    soft = jnp.maximum(shifted, 0.0) + log1p_exact(jnp.exp(-jnp.abs(shifted)))
    decays = rate_ref[0:1, :] * soft
    turn = lax.rem(BLOCK - head_start, BLOCK)
    beta_all = pltpu.roll(beta_all, turn, 1)
    decays = pltpu.roll(decays, turn, 1)
    tril = jnp.where(inclusive, 1.0, 0.0).astype(bf16)
    d0 = decays.astype(bf16)
    rest = decays - d0.astype(f32)
    d1 = rest.astype(bf16)
    d2 = (rest - d1.astype(f32)).astype(bf16)
    cum = jnp.dot(tril, d2, preferred_element_type=f32)
    cum = cum + jnp.dot(tril, d1, preferred_element_type=f32)
    cum = cum + jnp.dot(tril, d0, preferred_element_type=f32)
    cum_t = jnp.transpose(cum)

    queries, key_rows, kk, qk = [], [], [], []
    for g in range(keys):
        queries.append(unit(conv(g * HEAD_DIM)) * HEAD_DIM ** (-0.5))
        key_rows.append(unit(conv(wk + g * HEAD_DIM)))
        ks = split(key_rows[g])
        qs = split(queries[g])
        kk.append(mm(ks, ks, NT))
        qk.append(mm(qs, ks, NT))

    hs = range(heads)
    lower, scores, rhs, kdt, qd, last = [], [], [], [], [], []
    for h in hs:
        g = h * keys // heads
        beta = beta_all[:, h : h + 1]
        c = cum[:, VALUE_HEADS + h : VALUE_HEADS + h + 1]
        ct = cum_t[VALUE_HEADS + h : VALUE_HEADS + h + 1, :]
        final = ct[:, BLOCK - 1 :]
        spread = c - ct
        incl = jnp.where(inclusive, jnp.exp(jnp.where(inclusive, spread, 0.0)), 0.0)
        lower.append(jnp.where(strict, beta * kk[g] * incl, 0.0))
        scores.append(split(qk[g] * incl))
        grow = jnp.exp(c)
        values = conv(2 * wk + h * HEAD_DIM)
        rhs.append(split(jnp.concatenate([values * beta, key_rows[g] * (beta * grow)], axis=1)))
        kdt.append(split(jnp.transpose(key_rows[g] * jnp.exp(final - c))))
        qd.append(queries[g] * grow)
        last.append(jnp.exp(final))

    def same(size):
        return (row // size) == (col // size)

    small = 16
    power = [split(jnp.where(same(small), -lower[h], 0.0)) for h in hs]
    inverse = [eye + jnp.where(same(small), -lower[h], 0.0) for h in hs]
    steps = 1
    while 2**steps < small:
        power = [split(mm(power[h], power[h])) for h in hs]
        inverse = [inverse[h] + mm(split(inverse[h]), power[h]) for h in hs]
        steps += 1
    size = small
    while size < BLOCK:
        between = same(2 * size) & (~same(size))
        cross = [split(jnp.where(between, lower[h], 0.0)) for h in hs]
        parts = [split(inverse[h]) for h in hs]
        mixed = [split(mm(cross[h], parts[h])) for h in hs]
        inverse = [inverse[h] - mm(parts[h], mixed[h]) for h in hs]
        size *= 2
    solved = [split(mm(split(inverse[h]), rhs[h])) for h in hs]
    outs = [mm(scores[h], solved[h]) for h in hs]
    ends = [mm(kdt[h], solved[h]) for h in hs]
    states = [split(st_ref[h]) for h in hs]
    readers = [split(qd[h] - outs[h][:, HEAD_DIM:]) for h in hs]
    maps = [split(last[h] * eye - ends[h][:, HEAD_DIM:]) for h in hs]
    for h in hs:
        seen = mm(readers[h], states[h])
        o_ref[h] = seen[:, :HEAD_DIM] + outs[h][:, :HEAD_DIM]
        m_ref[h] = seen[:, HEAD_DIM:]
    for h in hs:
        moved = mm(maps[h], states[h])
        new = jnp.concatenate([moved[:, :HEAD_DIM] + ends[h][:, :HEAD_DIM], moved[:, HEAD_DIM:]], axis=1)
        st_ref[h] = new
        end_ref[h] = new


def local_terms(heads, meta, q, k, v, g, tail, weights, rates):
    count = q.shape[0] // 2
    seq = count * BLOCK

    def whole(x):
        return pl.BlockSpec(x.shape, lambda b, m, nd=x.ndim: (0,) * nd)

    def per_block():
        return pl.BlockSpec((heads, BLOCK, HEAD_DIM), lambda b, m: (0, b, 0))

    dots = 40 * heads * count
    return pl.pallas_call(
        functools.partial(local_kernel, heads),
        grid_spec=pltpu.PrefetchScalarGridSpec(
            num_scalar_prefetch=1,
            grid=(count,),
            in_specs=[whole(x) for x in (q, k, v, g, tail, weights, rates)],
            out_specs=[
                per_block(),
                per_block(),
                pl.BlockSpec((heads, HEAD_DIM, 2 * HEAD_DIM), lambda b, m: (0, 0, 0)),
            ],
            scratch_shapes=[
                pltpu.VMEM((BLOCK + 8, weights.shape[1]), f32),
                pltpu.VMEM((heads, HEAD_DIM, 2 * HEAD_DIM), f32),
            ],
        ),
        out_shape=(
            jax.ShapeDtypeStruct((heads, seq, HEAD_DIM), f32),
            jax.ShapeDtypeStruct((heads, seq, HEAD_DIM), f32),
            jax.ShapeDtypeStruct((heads, HEAD_DIM, 2 * HEAD_DIM), f32),
        ),
        compiler_params=pltpu.CompilerParams(
            dimension_semantics=("arbitrary",), vmem_limit_bytes=60 * 1024 * 1024
        ),
        cost_estimate=pl.CostEstimate(
            flops=6 * dots * BLOCK**3, bytes_accessed=12 * seq * heads * HEAD_DIM, transcendentals=0
        ),
        name="local_terms",
    )(meta, q, k, v, g, tail, weights, rates)


def chain_kernel(segs, heads, end_ref, inc_ref, out_ref, send, recv):
    seg = lax.axis_index("seg")
    me = lax.axis_index("cp")
    barrier = pltpu.get_barrier_semaphore()

    @pl.when(seg > 0)
    def _():
        pl.semaphore_signal(barrier, inc=1, device_id=(seg - 1, me), device_id_type=MESH)

    @pl.when(seg < segs - 1)
    def _():
        pl.semaphore_wait(barrier, 1)

    def hop(h):
        return pltpu.make_async_remote_copy(
            src_ref=out_ref.at[h],
            dst_ref=inc_ref.at[h],
            send_sem=send.at[h],
            recv_sem=recv.at[h],
            device_id=(lax.rem(seg + 1, segs), me),
            device_id_type=MESH,
        )

    for h in range(heads):
        @pl.when(seg == 0)
        def _():
            inc_ref[h] = jnp.zeros((HEAD_DIM, HEAD_DIM), f32)
            out_ref[h] = end_ref[h, :, :HEAD_DIM]

        @pl.when(seg > 0)
        def _():
            hop(h).wait_recv()

            @pl.when(seg < segs - 1)
            def _():
                out_ref[h] = end_ref[h, :, :HEAD_DIM] + mm(
                    split(end_ref[h, :, HEAD_DIM:]), split(inc_ref[h])
                )

        @pl.when(seg < segs - 1)
        def _():
            hop(h).start()

    for h in range(heads):
        @pl.when(seg < segs - 1)
        def _():
            hop(h).wait_send()


def chain(segs, heads, ends):
    return pl.pallas_call(
        functools.partial(chain_kernel, segs, heads),
        out_shape=jax.ShapeDtypeStruct((heads, HEAD_DIM, HEAD_DIM), f32),
        in_specs=[pl.BlockSpec(memory_space=pltpu.VMEM)],
        out_specs=pl.BlockSpec(memory_space=pltpu.VMEM),
        scratch_shapes=[
            pltpu.VMEM((heads, HEAD_DIM, HEAD_DIM), f32),
            pltpu.SemaphoreType.DMA((heads,)),
            pltpu.SemaphoreType.DMA((heads,)),
        ],
        compiler_params=pltpu.CompilerParams(collective_id=1, has_side_effects=True),
        name="chain",
    )(ends)


def finish_kernel(heads, meta, o_ref, m_ref, inc_ref, z_ref, gain_ref, y_ref):
    b = pl.program_id(0)
    i0 = meta[2 * b]
    i1 = meta[2 * b + 1]
    for h in range(heads):
        cols = slice(h * HEAD_DIM, (h + 1) * HEAD_DIM)
        core = o_ref[h] + mm(split(m_ref[h]), split(inc_ref[h]))
        z = jnp.concatenate([z_ref[i0, :, cols], z_ref[i1, :, cols]], axis=0).astype(f32)
        scale = lax.rsqrt(jnp.sum(core * core, axis=-1, keepdims=True) * (1.0 / HEAD_DIM) + 1e-06)
        y_ref[:, cols] = (core * scale * gain_ref[0:1, :] * (z / (1.0 + jnp.exp(-z)))).astype(bf16)


def finish(heads, meta, local_out, reach, incoming, z, gain):
    count = z.shape[0] // 2
    per_block = pl.BlockSpec((heads, BLOCK, HEAD_DIM), lambda b, m: (0, b, 0))
    return pl.pallas_call(
        functools.partial(finish_kernel, heads),
        grid_spec=pltpu.PrefetchScalarGridSpec(
            num_scalar_prefetch=1,
            grid=(count,),
            in_specs=[
                per_block,
                per_block,
                pl.BlockSpec(incoming.shape, lambda b, m: (0, 0, 0)),
                pl.BlockSpec(z.shape, lambda b, m: (0, 0, 0)),
                pl.BlockSpec(gain.shape, lambda b, m: (0, 0)),
            ],
            out_specs=pl.BlockSpec((BLOCK, heads * HEAD_DIM), lambda b, m: (b, 0)),
        ),
        out_shape=jax.ShapeDtypeStruct((count * BLOCK, heads * HEAD_DIM), bf16),
        compiler_params=pltpu.CompilerParams(dimension_semantics=("arbitrary",)),
        name="finish",
    )(meta, local_out, reach, incoming, z, gain)


def gather_kernel(n, y, out, send, recv, local):
    me = lax.axis_index("cp")
    seg = lax.axis_index("seg")
    rows = y.shape[0] // n
    width = y.shape[1]
    barrier = pltpu.get_barrier_semaphore()
    for d in range(1, n):
        pl.semaphore_signal(
            barrier, inc=1, device_id=(seg, lax.rem(me + d, n)), device_id_type=MESH
        )
    pl.semaphore_wait(barrier, n - 1)

    def src(p):
        return y.at[pl.ds(pl.multiple_of(p * rows, rows), rows), :]

    def dst(p):
        return out.at[:, pl.ds(pl.multiple_of(p * width, width), width)]

    started = []
    for d in range(1, n):
        peer = lax.rem(me + d, n)
        copy = pltpu.make_async_remote_copy(
            src_ref=src(peer),
            dst_ref=dst(me),
            send_sem=send.at[peer],
            recv_sem=recv.at[me],
            device_id=(seg, peer),
            device_id_type=MESH,
        )
        copy.start()
        started.append(copy)
    own = pltpu.make_async_copy(src(me), dst(me), local)
    own.start()
    own.wait()
    for d in range(1, n):
        source = lax.rem(me + n - d, n)
        pltpu.make_async_remote_copy(
            src_ref=src(me),
            dst_ref=dst(source),
            send_sem=send.at[source],
            recv_sem=recv.at[source],
            device_id=(seg, source),
            device_id_type=MESH,
        ).wait_recv()
    for copy in started:
        copy.wait_send()


def gather(n, y):
    return pl.pallas_call(
        functools.partial(gather_kernel, n),
        out_shape=jax.ShapeDtypeStruct((y.shape[0] // n, y.shape[1] * n), y.dtype),
        in_specs=[pl.BlockSpec(memory_space=pltpu.VMEM)],
        out_specs=pl.BlockSpec(memory_space=pltpu.VMEM),
        scratch_shapes=[
            pltpu.SemaphoreType.DMA((n,)),
            pltpu.SemaphoreType.DMA((n,)),
            pltpu.SemaphoreType.DMA,
        ],
        compiler_params=pltpu.CompilerParams(collective_id=2, has_side_effects=True),
        name="gather",
    )(y)


def per_device(mixed_qkv, gate_z, gate_logits, block_table, conv_weight, a_log, dt_bias, norm_gain):
    n = lax.axis_size("cp")
    segs = lax.axis_size("seg")
    me = lax.axis_index("cp")
    seg = lax.axis_index("seg")
    heads = VALUE_HEADS // n
    keys = max(1, heads // GROUP)
    wk, wv = keys * HEAD_DIM, heads * HEAD_DIM
    key_width = KEY_HEADS * HEAD_DIM
    blocks = 2 * n

    prior_table = lax.ppermute(block_table, "seg", [(i, (i + 1) % segs) for i in range(segs)])
    places = jnp.arange(blocks, dtype=jnp.int32)
    order = jnp.sum(
        jnp.where(block_table[0][None, :] == places[:, None], places[None, :], 0), axis=1, dtype=jnp.int32
    )
    tail_from = jnp.sum(jnp.where(prior_table[0] == blocks - 1, places, 0), dtype=jnp.int32) // 2
    meta = jnp.concatenate(
        [order, jnp.stack([tail_from, (seg == 0).astype(jnp.int32), (me * heads).astype(jnp.int32)])]
    )
    kcol = me * heads // GROUP * HEAD_DIM
    weights = jnp.concatenate(
        [
            lax.dynamic_slice_in_dim(conv_weight, kcol, wk, 1),
            lax.dynamic_slice_in_dim(conv_weight, key_width + kcol, wk, 1),
            lax.dynamic_slice_in_dim(conv_weight, 2 * key_width + me * wv, wv, 1),
        ],
        axis=1,
    )
    spare = HEAD_DIM - 2 * VALUE_HEADS
    rates = jnp.stack(
        [jnp.pad(-jnp.exp(a_log), (VALUE_HEADS, spare)), jnp.pad(dt_bias, (VALUE_HEADS, spare))]
    )
    q, k, v, z, g, tail = scatter(n, segs, heads, mixed_qkv, gate_z, gate_logits)

    def stored(x):
        return x.reshape(blocks, x.shape[1] // 2, x.shape[2])

    local_out, reach, ends = local_terms(
        heads, meta, stored(q), stored(k), stored(v), stored(g), tail, weights, rates
    )
    incoming = chain(segs, heads, ends)
    y = finish(heads, meta, local_out, reach, incoming, stored(z), norm_gain[None, :])
    return gather(n, y)


def solution(mesh):
    return jax.shard_map(
        per_device,
        mesh=mesh,
        in_specs=(
            P(("seg", "cp"), None),
            P(("seg", "cp"), None),
            P(("seg", "cp"), None),
            P("seg", None),
            P(),
            P(),
            P(),
            P(),
        ),
        out_specs=P(("seg", "cp"), None),
        check_vma=False,
    )
```

profile of v0, /device:TPU:17, one launch (start us, length us, event | category | flops | bytes accessed | tf_op | source)
XLA Modules:
  0.0 138.8 jit_solution(24728362864309553)
XLA Ops:
  0.0 1.3 collective-permute-start
  1.3 0.7 exponential_negate_fusion
  2.0 0.8 select_reduce_fusion
  2.7 1.4 %copy.10.gates = bf16[128,64]{1,0:T(8,128)(2,1)} copy(bf16[128,64]{0,1:T(8,128)(2,1)} %param.10) | data formatting | bytes 32768 | tf_op args[2]
  4.2 0.7 pad_bitcast_fusion
  4.9 0.6 pad_maximum_fusion.1.rate_ref
  5.5 0.7 constant_dynamic-slice_fusion
  6.2 0.7 constant_dynamic-slice_fusion.2
  6.9 0.6 pad_maximum_fusion.w_ref
  7.5 47.0 %scatter.1 = (bf16[8,128,256]{2,1,0:T(8,128)(2,1)}, bf16[8,128,256]{2,1,0:T(8,128)(2,1)}, bf16[8,128,512]{2,1,0:T(8,128)(2,1)}, bf16[8,128,512]{2,1,0:T(8,128)(2...) custom-call(bf16[128,8192]{1,0:T(8,128)(2,1)} %qkv.1, bf16[128,4096]{1,0:T(8,128)(2,1)} %z.1, ...), custom_call_target="tpu_custom_call" | custom-call | tf_op jit(solution)/shard_map/scatter/pallas_call | solution.py:140
  54.5 0.0 collective-permute-done
  54.5 0.6 fusion
  57.7 0.6 pad_add_fusion.meta
  58.3 36.3 %local_terms.1 = (f32[4,1024,128]{2,1,0:T(8,128)}, f32[4,1024,128]{2,1,0:T(8,128)}, f32[4,128,256]{2,1,0:T(8,128)}) custom-call(s32[19]{0:T(128)} %pad_add_fusion.meta, bf16[16,64,256]{2,1,0:T(8,128)(2,1)} %bitcast.21, bf16[16,64,256]{2,1,0:T(8,128)(2,1)} %bitcast.22, bf16[16,64,512]{2,1,0:T(8,128)(2,1)} %bitcast.20, bf16[16,64,64]{2,1,0:T(8,128)(2,1)} %bitcast.23, ...), custom_call_target="tpu_custom_call" | custom-call | flops 16106127360 | bytes 6291456 | tf_op jit(solution)/shard_map/local_terms/pallas_call | solution.py:308
  94.6 15.0 %chain.1.inc_ref = f32[4,128,128]{2,1,0:T(8,128)} custom-call(f32[4,128,256]{2,1,0:T(8,128)} %get-tuple-element.21.end_ref), custom_call_target="tpu_custom_call" | custom-call | tf_op jit(solution)/shard_map/chain/pallas_call | solution.py:389
  109.6 8.3 %finish.1.y = bf16[1024,512]{1,0:T(8,128)(2,1)} custom-call(s32[19]{0:T(128)} %pad_add_fusion.meta, f32[4,1024,128]{2,1,0:T(8,128)} %get-tuple-element.19.o_ref, f32[4,1024,128]{2,1,0:T(8,128)} %get-tuple-element.20.m_ref, f32[4,128,128]{2,1,0:T(8,128)} %chain.1.inc_ref, bf16[16,64,512]{2,1,0:T(8,128)(2,1)} %bitcast.18, f32[1,128]{1,0:T(1,128)} %bitcast.19), custom_call_target="tpu_custom_call" | custom-call | tf_op jit(solution)/shard_map/finish/pallas_call | solution.py:419
  117.8 18.7 %gather.1 = bf16[128,4096]{1,0:T(8,128)(2,1)} custom-call(bf16[1024,512]{1,0:T(8,128)(2,1)} %finish.1.y), custom_call_target="tpu_custom_call" | custom-call | tf_op jit(solution)/shard_map/gather/pallas_call | solution.py:488
  136.5 2.3 %copy.12 = bf16[128,4096]{1,0:T(8,128)(2,1)} copy(bf16[128,4096]{1,0:T(8,128)(2,1)} %gather.1) | data formatting | bytes 2097152
Async XLA Ops:
  0.0 54.5 %collective-permute-start = (s32[1,16]{1,0:T(1,128)}, s32[1,16]{1,0:T(1,128)S(1)}, u32[]{:S(2)}, u32[]{:S(2)}) collective-permute-start(s32[1,16]{1,0:T(1,128)} %param.11), channel_id=1, source_target_pairs={{0,8},{8,16},{16,24},{24,0},{1,9},{9,17},{17,25},{25,1},{2,10},{10... | collective-permute-start | bytes 200 | tf_op jit(solution)/shard_map/ppermute | solution.py:514
where the time goes:
time: 140 us; the launch traced here: 139 us
  Pallas kernels  125 us (89%)
  local copies, waits for them, and re-layouts  5.85 us (4%)
  other arithmetic  3.81 us (3%)
  between operations  2.65 us (2%)
    pallas_call x1, Pallas kernels, scatter(): pl.pallas_call(functools.partial(scatter_kernel, n, segs, heads), out_sha...  47 us
    pallas_call x1, Pallas kernels, local_terms(): pl.pallas_call(functools.partial(local_kernel, heads), grid_spec=pltpu.Pr...  36.3 us
    pallas_call x1, Pallas kernels, gather(): pl.pallas_call(functools.partial(gather_kernel, n), out_shape=jax.ShapeDt...  18.7 us
    pallas_call x1, Pallas kernels, chain(): pl.pallas_call(functools.partial(chain_kernel, segs, heads), out_shape=ja...  15 us
    pallas_call x1, Pallas kernels, finish(): pl.pallas_call(functools.partial(finish_kernel, heads), grid_spec=pltpu.P...  8.25 us
    unnamed x2, local copies, waits for them, and re-layouts  3.72 us
  transfers between devices with their start and end apart: 1, of which 0 were waited for; matrix products, arithmetic and copies ran while one was open for 4% of the time, Pallas kernels for 34%

commit v1 on v0

v1 whole, which is shorter than its diff:
```python
import functools

import jax
import jax.numpy as jnp
from jax import lax
from jax.experimental import pallas as pl
from jax.experimental.pallas import tpu as pltpu
from jax.sharding import PartitionSpec as P

VALUE_HEADS = 32
KEY_HEADS = 16
HEAD_DIM = 128
CONV = 4
BLOCK = 128
TAIL = 8
GROUP = VALUE_HEADS // KEY_HEADS

f32 = jnp.float32
bf16 = jnp.bfloat16
MESH = pl.DeviceIdType.MESH
highest = lax.Precision.HIGHEST


def split(x):
    hi = x.astype(bf16)
    return hi, (x - hi.astype(f32)).astype(bf16)


NN = (((1,), (0,)), ((), ()))
NT = (((1,), (1,)), ((), ()))


def mm(a, b, dims=NN):
    def dot(x, y):
        return lax.dot_general(x, y, dims, preferred_element_type=f32)

    return dot(a[0], b[0]) + (dot(a[0], b[1]) + dot(a[1], b[0]))


def log1p_exact(y):
    u = 1.0 + y
    return jnp.where(u == 1.0, y, jnp.log(u) * (y / jnp.where(u == 1.0, 1.0, u - 1.0)))


def block_step(
    heads, b, start, order, parts_now, first_prior, head_start, w_ref, rate_ref, o_ref, mh_ref, ml_ref, st_ref, x_ref
):
    keys = max(1, heads // GROUP)
    wk, wv = keys * HEAD_DIM, heads * HEAD_DIM
    i0 = order[2 * b] // 2
    i1 = order[2 * b + 1] // 2
    ip = order[jnp.maximum(2 * b - 1, 0)] // 2
    half = parts_now[0].shape[1]

    row = lax.broadcasted_iota(jnp.int32, (BLOCK, BLOCK), 0)
    col = lax.broadcasted_iota(jnp.int32, (BLOCK, BLOCK), 1)
    strict = row > col
    inclusive = row >= col
    eye = jnp.where(row == col, 1.0, 0.0).astype(f32)

    at = 0
    for place, width in enumerate((wk, wk, wv)):
        cols = slice(at, at + width)
        ref = parts_now[place]
        prior = ref[ip, half - 16 :, :].astype(f32)[8:]
        x_ref[0:8, cols] = jnp.where(b == start, first_prior(place, cols), prior)
        x_ref[8 : 8 + half, cols] = ref[i0].astype(f32)
        x_ref[8 + half : 8 + 2 * half, cols] = ref[i1].astype(f32)
        at += width

    def conv(start):
        cols = slice(start, start + HEAD_DIM)
        total_rows = w_ref[0:1, cols] * x_ref[5 : 5 + BLOCK, cols]
        for j in range(1, CONV):
            total_rows = total_rows + w_ref[j : j + 1, cols] * x_ref[5 + j : 5 + j + BLOCK, cols]
        return total_rows / (1.0 + jnp.exp(-total_rows))

    def unit(x):
        return x * lax.rsqrt(jnp.sum(x * x, axis=-1, keepdims=True) + 1e-06)

    gates = jnp.concatenate([parts_now[3][i0], parts_now[3][i1]], axis=0).astype(f32)
    gates = jnp.concatenate([gates, jnp.zeros((BLOCK, BLOCK - gates.shape[1]), f32)], axis=1)
    beta_all = 1.0 / (1.0 + jnp.exp(-gates))
    shifted = gates + rate_ref[1:2, :]
    soft = jnp.maximum(shifted, 0.0) + log1p_exact(jnp.exp(-jnp.abs(shifted)))
    decays = rate_ref[0:1, :] * soft
    turn = lax.rem(BLOCK - head_start, BLOCK)
    beta_all = pltpu.roll(beta_all, turn, 1)
    decays = pltpu.roll(decays, turn, 1)
    tril = jnp.where(inclusive, 1.0, 0.0).astype(bf16)
    d0 = decays.astype(bf16)
    rest = decays - d0.astype(f32)
    d1 = rest.astype(bf16)
    d2 = (rest - d1.astype(f32)).astype(bf16)
    cum = jnp.dot(tril, d2, preferred_element_type=f32)
    cum = cum + jnp.dot(tril, d1, preferred_element_type=f32)
    cum = cum + jnp.dot(tril, d0, preferred_element_type=f32)
    cum_t = jnp.transpose(cum)

    queries, key_rows, kk, qk = [], [], [], []
    for g in range(keys):
        queries.append(unit(conv(g * HEAD_DIM)) * HEAD_DIM ** (-0.5))
        key_rows.append(unit(conv(wk + g * HEAD_DIM)))
        ks = split(key_rows[g])
        qs = split(queries[g])
        kk.append(mm(ks, ks, NT))
        qk.append(mm(qs, ks, NT))

    hs = range(heads)
    lower, scores, rhs, kdt, qd, last = [], [], [], [], [], []
    for h in hs:
        g = h * keys // heads
        beta = beta_all[:, h : h + 1]
        c = cum[:, VALUE_HEADS + h : VALUE_HEADS + h + 1]
        ct = cum_t[VALUE_HEADS + h : VALUE_HEADS + h + 1, :]
        final = ct[:, BLOCK - 1 :]
        spread = c - ct
        incl = jnp.where(inclusive, jnp.exp(jnp.where(inclusive, spread, 0.0)), 0.0)
        lower.append(jnp.where(strict, beta * kk[g] * incl, 0.0))
        scores.append(split(qk[g] * incl))
        grow = jnp.exp(c)
        values = conv(2 * wk + h * HEAD_DIM)
        rhs.append(split(jnp.concatenate([values * beta, key_rows[g] * (beta * grow)], axis=1)))
        kdt.append(split(jnp.transpose(key_rows[g] * jnp.exp(final - c))))
        qd.append(queries[g] * grow)
        last.append(jnp.exp(final))

    def same(size):
        return (row // size) == (col // size)

    small = 16
    power = [split(jnp.where(same(small), -lower[h], 0.0)) for h in hs]
    inverse = [eye + jnp.where(same(small), -lower[h], 0.0) for h in hs]
    steps = 1
    while 2**steps < small:
        power = [split(mm(power[h], power[h])) for h in hs]
        inverse = [inverse[h] + mm(split(inverse[h]), power[h]) for h in hs]
        steps += 1
    size = small
    while size < BLOCK:
        between = same(2 * size) & (~same(size))
        cross = [split(jnp.where(between, lower[h], 0.0)) for h in hs]
        parts = [split(inverse[h]) for h in hs]
        mixed = [split(mm(cross[h], parts[h])) for h in hs]
        inverse = [inverse[h] - mm(parts[h], mixed[h]) for h in hs]
        size *= 2
    solved = [split(mm(split(inverse[h]), rhs[h])) for h in hs]
    outs = [mm(scores[h], solved[h]) for h in hs]
    ends = [mm(kdt[h], solved[h]) for h in hs]
    states = [split(st_ref[h]) for h in hs]
    readers = [split(qd[h] - outs[h][:, HEAD_DIM:]) for h in hs]
    maps = [split(last[h] * eye - ends[h][:, HEAD_DIM:]) for h in hs]
    for h in hs:
        seen = mm(readers[h], states[h])
        o_ref[h, b] = seen[:, :HEAD_DIM] + outs[h][:, :HEAD_DIM]
        reach = split(seen[:, HEAD_DIM:])
        mh_ref[h, b] = reach[0]
        ml_ref[h, b] = reach[1]
    for h in hs:
        moved = mm(maps[h], states[h])
        new = jnp.concatenate([moved[:, :HEAD_DIM] + ends[h][:, :HEAD_DIM], moved[:, HEAD_DIM:]], axis=1)
        st_ref[h] = new


def mix_kernel(
    n, segs, heads, order, qkv, z, gates, conv_weight, rate_ref, o_ref, mh_ref, ml_ref, st_ref, oz,
    qa, ka, va, ga, qb, kb, vb, gb, otail, w_ref, x_ref, send, recv, local
):
    me = lax.axis_index("cp")
    seg = lax.axis_index("seg")
    after = lax.rem(seg + 1, segs)
    before = lax.rem(seg + segs - 1, segs)
    keys = max(1, heads // GROUP)
    wk, wv = keys * HEAD_DIM, heads * HEAD_DIM
    key_width = KEY_HEADS * HEAD_DIM
    rows = qkv.shape[0]
    half = rows // 2

    barrier = pltpu.get_barrier_semaphore()
    for d in range(n):
        peer = lax.rem(me + d, n)
        if d:
            pl.semaphore_signal(barrier, inc=1, device_id=(seg, peer), device_id_type=MESH)
        pl.semaphore_signal(barrier, inc=1, device_id=(before, peer), device_id_type=MESH)

    def columns(start, width):
        return pl.ds(pl.multiple_of(start, HEAD_DIM), width)

    def pieces(p, slot):
        kcol = lax.div(p * heads, GROUP) * HEAD_DIM
        vcol = p * wv
        found = []
        for first, bufs in ((0, (qa, ka, va, ga)), (half, (qb, kb, vb, gb))):
            these = pl.ds(first, half)
            found += [
                (qkv.at[these, columns(kcol, wk)], bufs[0].at[slot]),
                (qkv.at[these, columns(key_width + kcol, wk)], bufs[1].at[slot]),
                (qkv.at[these, columns(2 * key_width + vcol, wv)], bufs[2].at[slot]),
                (gates.at[these], bufs[3].at[slot]),
            ]
        return found + [(z.at[:, columns(vcol, wv)], oz.at[slot])]

    def tails(p, slot):
        kcol = lax.div(p * heads, GROUP) * HEAD_DIM
        vcol = p * wv
        last = pl.ds(rows - TAIL, TAIL)
        return [
            (qkv.at[last, columns(kcol, wk)], otail.at[slot, :, pl.ds(0, wk)]),
            (qkv.at[last, columns(key_width + kcol, wk)], otail.at[slot, :, pl.ds(wk, wk)]),
            (qkv.at[last, columns(2 * key_width + vcol, wv)], otail.at[slot, :, pl.ds(2 * wk, wv)]),
        ]

    own = []
    kcol = lax.div(me * heads, GROUP) * HEAD_DIM
    mine = pieces(me, me) + [
        (conv_weight.at[:, columns(kcol, wk)], w_ref.at[:, pl.ds(0, wk)]),
        (conv_weight.at[:, columns(key_width + kcol, wk)], w_ref.at[:, pl.ds(wk, wk)]),
        (conv_weight.at[:, columns(2 * key_width + me * wv, wv)], w_ref.at[:, pl.ds(2 * wk, wv)]),
    ]
    for kind, (src, dst) in enumerate(mine):
        copy = pltpu.make_async_copy(src, dst, local.at[kind])
        copy.start()
        own.append(copy)
    pl.semaphore_wait(barrier, 2 * n - 1)

    started = []

    def post(kind, src, dst, peer, target):
        copy = pltpu.make_async_remote_copy(
            src_ref=src,
            dst_ref=dst,
            send_sem=send.at[kind, peer],
            recv_sem=recv.at[kind, me],
            device_id=target,
            device_id_type=MESH,
        )
        copy.start()
        started.append(copy)

    for kinds in ((0, 1, 2, 3), (4, 5, 6, 7), (8,)):
        for d in range(1, n):
            peer = lax.rem(me + d, n)
            sources = pieces(peer, me)
            for kind in kinds:
                post(kind, *sources[kind], peer, (seg, peer))
        if kinds[0] == 0:
            for d in range(n):
                peer = lax.rem(me + d, n)
                for i, (src, dst) in enumerate(tails(peer, me)):
                    post(9 + i, src, dst, peer, (after, peer))

    def arrived(kinds):
        for d in range(n):
            source = lax.rem(me + n - d, n)
            found = pieces(me, source) + tails(me, source)
            for kind in kinds:
                if d or kind > 8:
                    src, dst = found[kind]
                    pltpu.make_async_remote_copy(
                        src_ref=src,
                        dst_ref=dst,
                        send_sem=send.at[kind, source],
                        recv_sem=recv.at[kind, source],
                        device_id=(seg, source),
                        device_id_type=MESH,
                    ).wait_recv()

    row = lax.broadcasted_iota(jnp.int32, (HEAD_DIM, HEAD_DIM), 0)
    col = lax.broadcasted_iota(jnp.int32, (HEAD_DIM, HEAD_DIM), 1)
    for h in range(heads):
        st_ref[h, :, :HEAD_DIM] = jnp.zeros((HEAD_DIM, HEAD_DIM), f32)
        st_ref[h, :, HEAD_DIM:] = jnp.where(row == col, 1.0, 0.0).astype(f32)
    for copy in own:
        copy.wait()
    tail_from = order[2 * n]
    joint = order[n - 1] // 2
    early = (qa, ka, va, ga)
    late = (qb, kb, vb, gb)

    def from_tail(place, cols):
        return jnp.where(seg == 0, 0.0, otail[tail_from].astype(f32)[:, cols])

    def from_early(place, cols):
        return early[place][joint, half - 16 :, :].astype(f32)[8:]

    def run(first, stop, bufs, prior):
        def one(b, carry):
            block_step(
                heads, b, first, order, bufs, prior, me * heads,
                w_ref, rate_ref, o_ref, mh_ref, ml_ref, st_ref, x_ref,
            )
            return carry

        lax.fori_loop(first, stop, one, 0)

    arrived((0, 1, 2, 3, 9, 10, 11))
    run(0, n // 2, early, from_tail)
    arrived((4, 5, 6, 7))
    run(n // 2, n, late, from_early)
    arrived((8,))
    for copy in started:
        copy.wait_send()


def mix(n, segs, heads, order, qkv, z, gates, conv_weight, rates):
    keys = max(1, heads // GROUP)
    wk, wv = keys * HEAD_DIM, heads * HEAD_DIM
    rows = qkv.shape[0]
    half = rows // 2
    anywhere = pl.BlockSpec(memory_space=pl.ANY)
    vmem = pl.BlockSpec(memory_space=pltpu.VMEM)
    widths = (wk, wk, wv, gates.shape[1])
    return pl.pallas_call(
        functools.partial(mix_kernel, n, segs, heads),
        out_shape=(
            jax.ShapeDtypeStruct((heads, n, BLOCK, HEAD_DIM), f32),
            jax.ShapeDtypeStruct((heads, n, BLOCK, HEAD_DIM), bf16),
            jax.ShapeDtypeStruct((heads, n, BLOCK, HEAD_DIM), bf16),
            jax.ShapeDtypeStruct((heads, HEAD_DIM, 2 * HEAD_DIM), f32),
            jax.ShapeDtypeStruct((n, rows, wv), bf16),
        ),
        in_specs=[pl.BlockSpec(memory_space=pltpu.SMEM)] + [anywhere] * 4 + [vmem],
        out_specs=[vmem] * 5,
        scratch_shapes=[pltpu.VMEM((n, half, w), bf16) for w in widths]
        + [pltpu.VMEM((n, half, w), bf16) for w in widths]
        + [
            pltpu.VMEM((n, TAIL, 2 * wk + wv), bf16),
            pltpu.VMEM((CONV, 2 * wk + wv), f32),
            pltpu.VMEM((BLOCK + 8, 2 * wk + wv), f32),
            pltpu.SemaphoreType.DMA((12, n)),
            pltpu.SemaphoreType.DMA((12, n)),
            pltpu.SemaphoreType.DMA((12,)),
        ],
        compiler_params=pltpu.CompilerParams(
            collective_id=0, has_side_effects=True, vmem_limit_bytes=40 * 1024 * 1024
        ),
        name="mix",
    )(order, qkv, z, gates, conv_weight, rates)


def close_kernel(
    n, segs, heads, order, end_ref, o_ref, mh_ref, ml_ref, z_ref, gain_ref, out,
    inc_ref, pass_ref, y_ref, send, recv, ysend, yrecv, local
):
    seg = lax.axis_index("seg")
    me = lax.axis_index("cp")
    final = segs - 1
    width = heads * HEAD_DIM
    barrier = pltpu.get_barrier_semaphore()
    for d in range(1, n):
        pl.semaphore_signal(
            barrier, inc=1, device_id=(seg, lax.rem(me + d, n)), device_id_type=MESH
        )
    pl.semaphore_signal(
        barrier, inc=1, device_id=(lax.rem(seg + segs - 1, segs), me), device_id_type=MESH
    )
    pl.semaphore_wait(barrier, n)

    def hop(h):
        return pltpu.make_async_remote_copy(
            src_ref=pass_ref.at[h],
            dst_ref=inc_ref.at[h],
            send_sem=send.at[h],
            recv_sem=recv.at[h],
            device_id=(lax.rem(seg + 1, segs), me),
            device_id_type=MESH,
        )

    @pl.when(seg == 0)
    def _():
        for h in range(heads):
            inc_ref[h] = jnp.zeros((HEAD_DIM, HEAD_DIM), f32)
            pass_ref[h] = end_ref[h, :, :HEAD_DIM]
        for h in range(heads):
            hop(h).start()

    @pl.when((seg > 0) & (seg < final))
    def _():
        for h in range(heads):
            through = split(end_ref[h, :, HEAD_DIM:])
            hop(h).wait_recv()
            pass_ref[h] = end_ref[h, :, :HEAD_DIM] + mm(through, split(inc_ref[h]))
            hop(h).start()

    def block(h, b, state):
        cols = pl.ds(h * HEAD_DIM, HEAD_DIM)
        i0 = order[2 * b]
        i1 = order[2 * b + 1]
        core = o_ref[h, b] + mm((mh_ref[h, b], ml_ref[h, b]), state)
        z = jnp.concatenate([z_ref[i0, :, cols], z_ref[i1, :, cols]], axis=0).astype(f32)
        scale = lax.rsqrt(jnp.sum(core * core, axis=-1, keepdims=True) * (1.0 / HEAD_DIM) + 1e-06)
        y_ref[h, b] = (core * scale * gain_ref[0:1, :] * (z / (1.0 + jnp.exp(-z)))).astype(bf16)

    def target(h, source):
        return out.at[:, pl.ds(pl.multiple_of(source * width + h * HEAD_DIM, HEAD_DIM), HEAD_DIM)]

    def give(h, d):
        peer = lax.rem(me + d, n)
        return pltpu.make_async_remote_copy(
            src_ref=y_ref.at[h, peer],
            dst_ref=target(h, me),
            send_sem=ysend.at[h, peer],
            recv_sem=yrecv.at[h, me],
            device_id=(seg, peer),
            device_id_type=MESH,
        )

    for h in range(heads):
        @pl.when(seg == final)
        def _():
            hop(h).wait_recv()

        state = split(inc_ref[h])

        for d in range(1, n):
            block(h, lax.rem(me + d, n), state)
            if d > 1:
                give(h, d - 1).start()
        block(h, me, state)
        give(h, n - 1).start()
        if h:
            pltpu.make_async_copy(y_ref.at[h - 1, me], target(h - 1, me), local.at[h - 1]).start()
    pltpu.make_async_copy(y_ref.at[heads - 1, me], target(heads - 1, me), local.at[heads - 1]).start()

    for h in range(heads):
        pltpu.make_async_copy(y_ref.at[h, me], target(h, me), local.at[h]).wait()
        for d in range(1, n):
            source = lax.rem(me + n - d, n)
            pltpu.make_async_remote_copy(
                src_ref=y_ref.at[h, source],
                dst_ref=target(h, source),
                send_sem=ysend.at[h, source],
                recv_sem=yrecv.at[h, source],
                device_id=(seg, source),
                device_id_type=MESH,
            ).wait_recv()
    for h in range(heads):
        for d in range(1, n):
            give(h, d).wait_send()

        @pl.when(seg < final)
        def _():
            hop(h).wait_send()


def close(n, segs, heads, order, ends, o, mh, ml, z, gain):
    vmem = pl.BlockSpec(memory_space=pltpu.VMEM)
    return pl.pallas_call(
        functools.partial(close_kernel, n, segs, heads),
        out_shape=jax.ShapeDtypeStruct((BLOCK, n * heads * HEAD_DIM), bf16),
        in_specs=[pl.BlockSpec(memory_space=pltpu.SMEM)] + [vmem] * 6,
        out_specs=vmem,
        scratch_shapes=[
            pltpu.VMEM((heads, HEAD_DIM, HEAD_DIM), f32),
            pltpu.VMEM((heads, HEAD_DIM, HEAD_DIM), f32),
            pltpu.VMEM((heads, n, BLOCK, HEAD_DIM), bf16),
            pltpu.SemaphoreType.DMA((heads,)),
            pltpu.SemaphoreType.DMA((heads,)),
            pltpu.SemaphoreType.DMA((heads, n)),
            pltpu.SemaphoreType.DMA((heads, n)),
            pltpu.SemaphoreType.DMA((heads,)),
        ],
        compiler_params=pltpu.CompilerParams(
            collective_id=1, has_side_effects=True, vmem_limit_bytes=40 * 1024 * 1024
        ),
        name="close",
    )(order, ends, o, mh, ml, z, gain)


def per_device(mixed_qkv, gate_z, gate_logits, block_table, conv_weight, a_log, dt_bias, norm_gain):
    n = lax.axis_size("cp")
    segs = lax.axis_size("seg")
    heads = VALUE_HEADS // n
    blocks = 2 * n

    prior_table = lax.ppermute(block_table, "seg", [(i, (i + 1) % segs) for i in range(segs)])
    places = jnp.arange(blocks, dtype=jnp.int32)
    order = jnp.sum(
        jnp.where(block_table[0][None, :] == places[:, None], places[None, :], 0), axis=1, dtype=jnp.int32
    )
    tail_from = jnp.sum(jnp.where(prior_table[0] == blocks - 1, places, 0), dtype=jnp.int32) // 2
    order = jnp.concatenate([order, tail_from[None]])
    spare = HEAD_DIM - 2 * VALUE_HEADS
    rates = jnp.stack(
        [jnp.pad(-jnp.exp(a_log), (VALUE_HEADS, spare)), jnp.pad(dt_bias, (VALUE_HEADS, spare))]
    )
    o, mh, ml, ends, z = mix(
        n, segs, heads, order, mixed_qkv, gate_z, gate_logits, conv_weight, rates
    )
    z = z.reshape(blocks, z.shape[1] // 2, z.shape[2])
    return close(n, segs, heads, order, ends, o, mh, ml, z, norm_gain[None, :])


def solution(mesh):
    return jax.shard_map(
        per_device,
        mesh=mesh,
        in_specs=(
            P(("seg", "cp"), None),
            P(("seg", "cp"), None),
            P(("seg", "cp"), None),
            P("seg", None),
            P(),
            P(),
            P(),
            P(),
        ),
        out_specs=P(("seg", "cp"), None),
        check_vma=False,
    )
```

time: 140 us -> 94.5 us (0.68)
  Pallas kernels: 125 us -> 81.8 us
  other arithmetic: 3.81 us -> 2.15 us
    pallas_call x5 -> x2, Pallas kernels: 125 us -> 81.8 us  [the longest x1 54.3 us: mix(): pl.pallas_call(functools.partial(mix_kernel, n, segs, heads), out_shape=(...]
    unnamed x2 -> x10, local copies, waits for them, and re-layouts: 3.72 us -> 5.52 us
    dynamic_slice x2 -> x0, local copies, waits for them, and re-layouts: 1.4 us -> none  [the longest x1 0.7 us: per_device(): lax.dynamic_slice_in_dim(conv_weight, kcol, wk, 1)]
  transfers between devices with their start and end apart: 1 -> 1, of which waited for: 0 -> 0; matrix products, arithmetic and copies ran while one was open for 4% -> 3% of each run, Pallas kernels for 34% -> 0%
where the time goes in v1:
time: 94.5 us; the launch traced here: 94.2 us
  Pallas kernels  81.8 us (87%)
  local copies, waits for them, and re-layouts  6.25 us (7%)
  between operations  2.65 us (3%)
  other arithmetic  2.15 us (2%)
  starting transfers between devices  1.3 us (1%)
    pallas_call x1, Pallas kernels, mix(): pl.pallas_call(functools.partial(mix_kernel, n, segs, heads), out_shape=(...  54.3 us
    pallas_call x1, Pallas kernels, close(): pl.pallas_call(functools.partial(close_kernel, n, segs, heads), out_shape...  27.5 us
    unnamed x10, local copies, waits for them, and re-layouts  5.52 us
  transfers between devices with their start and end apart: 1, of which 0 were waited for; matrix products, arithmetic and copies ran while one was open for 3% of the time, Pallas kernels for 0%

profile of v1, /device:TPU:17, one launch (start us, length us, event | category | flops | bytes accessed | tf_op | source)
XLA Modules:
  0.0 94.2 jit_solution(2189789214747852351)
XLA Ops:
  0.0 0.0 copy-start.3
  0.0 1.3 %collective-permute-start = (s32[1,16]{1,0:T(1,128)}, s32[1,16]{1,0:T(1,128)S(1)}, u32[]{:S(2)}, u32[]{:S(2)}) collective-permute-start(s32[1,16]{1,0:T(1,128)} %param.11), channel_id=1, source_target_pairs={{0,8},{8,16},{16,24},{24,0},{1,9},{9,17},{17,25},{25,1},{2,10},{10... | collective-permute-start | bytes 200 | tf_op jit(solution)/shard_map/ppermute | solution.py:476
  1.3 0.7 exponential_negate_fusion
  2.0 0.8 select_reduce_fusion
  2.7 0.7 pad_bitcast_fusion
  3.5 0.8 copy.10.gates
  4.3 0.0 collective-permute-done
  4.3 0.6 fusion
  7.6 0.1 pad_add_fusion.order
  7.6 0.0 copy-start
  7.6 1.6 %copy-done = bf16[128,8192]{1,0:T(8,128)(2,1)S(1)} copy-done((bf16[128,8192]{1,0:T(8,128)(2,1)S(1)}, bf16[128,8192]{1,0:T(8,128)(2,1)}, u32[]{:S(2)}) %copy-start) | copy-done | bytes 2097176
  9.2 0.0 copy-start.1
  9.2 1.2 %copy-done.1 = bf16[128,4096]{1,0:T(8,128)(2,1)S(1)} copy-done((bf16[128,4096]{1,0:T(8,128)(2,1)S(1)}, bf16[128,4096]{1,0:T(8,128)(2,1)}, u32[]{:S(2)}) %copy-start.1) | copy-done | bytes 1048600
  10.4 0.0 copy-start.2
  10.4 0.9 copy-done.2
  11.4 54.3 %mix.1 = (f32[4,8,128,128]{3,2,1,0:T(8,128)S(1)}, bf16[4,8,128,128]{3,2,1,0:T(8,128)(2,1)S(1)}, bf16[4,8,128,128]{3,2,1,0:T(8,128)(2,1)S(1)}, f32[4,128,256]{2,1,0:T(8,128)S(1)}, bf16[8,128,512]{2,1,0:T(8,128)(2,1)S(1)}) custom-call(s32[17]{0:T(128)S(1)} %pad_add_fusion.order, bf16[128,8192]{1,0:T(8,128)(2,1)S(1)} %copy-done, ...), custom_call_target="tpu_custom_call" | custom-call | tf_op jit(solution)/shard_map/mix/pallas_call | solution.py:313
  65.7 0.0 copy-done.3
  65.7 27.5 %close.1 = bf16[128,4096]{1,0:T(8,128)(2,1)S(1)} custom-call(s32[17]{0:T(128)S(1)} %pad_add_fusion.order, f32[4,128,256]{2,1,0:T(8,128)S(1)} %get-tuple-element.10.end_ref, f32[4,8,128,128]{3,2,1,0:T(8,128)S(1)} %get-tuple-element.11.o_ref, bf16[4,8,128,128]{3,2,1,0:T(8,128)(2,1)S(1)} %get-tuple-element.12.mh_ref, ...), custom_call_target="tpu_custom_call" | custom-call | tf_op jit(solution)/shard_map/close/pallas_call | solution.py:448
  93.2 1.0 %copy.12 = bf16[128,4096]{1,0:T(8,128)(2,1)} copy(bf16[128,4096]{1,0:T(8,128)(2,1)S(1)} %close.1) | data formatting | bytes 2097152
  (1 shorter events, 0.0 us)
Async XLA Ops:
  0.0 65.7 %copy-start.3 = (f32[128]{0:T(128)S(1)}, f32[128]{0:T(128)}, u32[]{:S(2)}) copy-start(f32[128]{0:T(128)} %param.15) | copy-start | bytes 1540
  0.0 4.3 %collective-permute-start = (s32[1,16]{1,0:T(1,128)}, s32[1,16]{1,0:T(1,128)S(1)}, u32[]{:S(2)}, u32[]{:S(2)}) collective-permute-start(s32[1,16]{1,0:T(1,128)} %param.11), channel_id=1, source_target_pairs={{0,8},{8,16},{16,24},{24,0},{1,9},{9,17},{17,25},{25,1},{2,10},{10... | collective-permute-start | bytes 200 | tf_op jit(solution)/shard_map/ppermute | solution.py:476
  7.6 1.6 %copy-start = (bf16[128,8192]{1,0:T(8,128)(2,1)S(1)}, bf16[128,8192]{1,0:T(8,128)(2,1)}, u32[]{:S(2)}) copy-start(bf16[128,8192]{1,0:T(8,128)(2,1)} %qkv.1) | copy-start | bytes 6291460
  9.2 1.2 %copy-start.1 = (bf16[128,4096]{1,0:T(8,128)(2,1)S(1)}, bf16[128,4096]{1,0:T(8,128)(2,1)}, u32[]{:S(2)}) copy-start(bf16[128,4096]{1,0:T(8,128)(2,1)} %z.1) | copy-start | bytes 3145732
  10.4 0.9 copy-start.2

commit v2 on v1

--- a/solution.py
+++ b/solution.py
@@ -14,6 +14,7 @@
 BLOCK = 128
 TAIL = 8
 GROUP = VALUE_HEADS // KEY_HEADS
+PAIR = 2
 
 f32 = jnp.float32
 bf16 = jnp.bfloat16
@@ -34,7 +35,15 @@
     def dot(x, y):
         return lax.dot_general(x, y, dims, preferred_element_type=f32)
 
-    return dot(a[0], b[0]) + (dot(a[0], b[1]) + dot(a[1], b[0]))
+    if dims == NT:
+        return dot(a[0], b[0]) + (dot(a[0], b[1]) + dot(a[1], b[0]))
+    wide = jnp.concatenate(a, axis=1)
+    if b[0].shape[1] > HEAD_DIM:
+        return dot(wide, jnp.concatenate([b[0], b[0]], axis=0)) + dot(a[0], b[1])
+    top = jnp.concatenate([b[0], b[1]], axis=1)
+    low = jnp.concatenate([b[0], jnp.zeros_like(b[1])], axis=1)
+    both = dot(wide, jnp.concatenate([top, low], axis=0))
+    return both[:, :HEAD_DIM] + both[:, HEAD_DIM:]
 
 
 def log1p_exact(y):
@@ -42,8 +51,8 @@
     return jnp.where(u == 1.0, y, jnp.log(u) * (y / jnp.where(u == 1.0, 1.0, u - 1.0)))
 
 
-def block_step(
-    heads, b, start, order, parts_now, first_prior, head_start, w_ref, rate_ref, o_ref, mh_ref, ml_ref, st_ref, x_ref
+def prepare(
+    heads, b, start, order, parts_now, first_prior, head_start, w_ref, rate_ref, x_ref
 ):
     keys = max(1, heads // GROUP)
     wk, wv = keys * HEAD_DIM, heads * HEAD_DIM
@@ -124,6 +133,24 @@
         kdt.append(split(jnp.transpose(key_rows[g] * jnp.exp(final - c))))
         qd.append(queries[g] * grow)
         last.append(jnp.exp(final))
+
+    return lower, scores, rhs, kdt, qd, last
+
+
+def block_pair(
+    heads, pair, start, order, parts_now, first_prior, head_start, w_ref, rate_ref, o_ref, mh_ref, ml_ref, st_ref, x_ref
+):
+    row = lax.broadcasted_iota(jnp.int32, (BLOCK, BLOCK), 0)
+    col = lax.broadcasted_iota(jnp.int32, (BLOCK, BLOCK), 1)
+    eye = jnp.where(row == col, 1.0, 0.0).astype(f32)
+    lower, scores, rhs, kdt, qd, last = [], [], [], [], [], []
+    for e in range(PAIR):
+        found = prepare(
+            heads, PAIR * pair + e, start, order, parts_now, first_prior, head_start, w_ref, rate_ref, x_ref.at[e]
+        )
+        for total, more in zip((lower, scores, rhs, kdt, qd, last), found):
+            total += more
+    hs = range(PAIR * heads)
 
     def same(size):
         return (row // size) == (col // size)
@@ -147,19 +174,24 @@
     solved = [split(mm(split(inverse[h]), rhs[h])) for h in hs]
     outs = [mm(scores[h], solved[h]) for h in hs]
     ends = [mm(kdt[h], solved[h]) for h in hs]
-    states = [split(st_ref[h]) for h in hs]
     readers = [split(qd[h] - outs[h][:, HEAD_DIM:]) for h in hs]
     maps = [split(last[h] * eye - ends[h][:, HEAD_DIM:]) for h in hs]
-    for h in hs:
-        seen = mm(readers[h], states[h])
-        o_ref[h, b] = seen[:, :HEAD_DIM] + outs[h][:, :HEAD_DIM]
-        reach = split(seen[:, HEAD_DIM:])
-        mh_ref[h, b] = reach[0]
-        ml_ref[h, b] = reach[1]
-    for h in hs:
-        moved = mm(maps[h], states[h])
-        new = jnp.concatenate([moved[:, :HEAD_DIM] + ends[h][:, :HEAD_DIM], moved[:, HEAD_DIM:]], axis=1)
-        st_ref[h] = new
+    for e in range(PAIR):
+        b = PAIR * pair + e
+        states = [split(st_ref[h]) for h in range(heads)]
+        for h in range(heads):
+            at = e * heads + h
+            moved = mm(maps[at], states[h])
+            st_ref[h] = jnp.concatenate(
+                [moved[:, :HEAD_DIM] + ends[at][:, :HEAD_DIM], moved[:, HEAD_DIM:]], axis=1
+            )
+        for h in range(heads):
+            at = e * heads + h
+            seen = mm(readers[at], states[h])
+            o_ref[h, b] = seen[:, :HEAD_DIM] + outs[at][:, :HEAD_DIM]
+            reach = split(seen[:, HEAD_DIM:])
+            mh_ref[h, b] = reach[0]
+            ml_ref[h, b] = reach[1]
 
 
 def mix_kernel(
@@ -198,7 +230,10 @@
                 (qkv.at[these, columns(2 * key_width + vcol, wv)], bufs[2].at[slot]),
                 (gates.at[these], bufs[3].at[slot]),
             ]
-        return found + [(z.at[:, columns(vcol, wv)], oz.at[slot])]
+        return found + [
+            (z.at[pl.ds(0, half), columns(vcol, wv)], oz.at[2 * slot]),
+            (z.at[pl.ds(half, half), columns(vcol, wv)], oz.at[2 * slot + 1]),
+        ]
 
     def tails(p, slot):
         kcol = lax.div(p * heads, GROUP) * HEAD_DIM
@@ -237,7 +272,7 @@
         copy.start()
         started.append(copy)
 
-    for kinds in ((0, 1, 2, 3), (4, 5, 6, 7), (8,)):
+    for kinds in ((0, 1, 2, 3), (4, 5, 6, 7), (8, 9)):
         for d in range(1, n):
             peer = lax.rem(me + d, n)
             sources = pieces(peer, me)
@@ -247,14 +282,14 @@
             for d in range(n):
                 peer = lax.rem(me + d, n)
                 for i, (src, dst) in enumerate(tails(peer, me)):
-                    post(9 + i, src, dst, peer, (after, peer))
+                    post(10 + i, src, dst, peer, (after, peer))
 
     def arrived(kinds):
         for d in range(n):
             source = lax.rem(me + n - d, n)
             found = pieces(me, source) + tails(me, source)
             for kind in kinds:
-                if d or kind > 8:
+                if d or kind > 9:
                     src, dst = found[kind]
                     pltpu.make_async_remote_copy(
                         src_ref=src,
@@ -285,57 +320,21 @@
 
     def run(first, stop, bufs, prior):
         def one(b, carry):
-            block_step(
+            block_pair(
                 heads, b, first, order, bufs, prior, me * heads,
                 w_ref, rate_ref, o_ref, mh_ref, ml_ref, st_ref, x_ref,
             )
             return carry
 
-        lax.fori_loop(first, stop, one, 0)
-
-    arrived((0, 1, 2, 3, 9, 10, 11))
+        lax.fori_loop(first // PAIR, stop // PAIR, one, 0)
+
+    arrived((0, 1, 2, 3, 10, 11, 12))
     run(0, n // 2, early, from_tail)
     arrived((4, 5, 6, 7))
     run(n // 2, n, late, from_early)
-    arrived((8,))
+    arrived((8, 9))
     for copy in started:
         copy.wait_send()
-
-
-def mix(n, segs, heads, order, qkv, z, gates, conv_weight, rates):
-    keys = max(1, heads // GROUP)
-    wk, wv = keys * HEAD_DIM, heads * HEAD_DIM
-    rows = qkv.shape[0]
-    half = rows // 2
-    anywhere = pl.BlockSpec(memory_space=pl.ANY)
-    vmem = pl.BlockSpec(memory_space=pltpu.VMEM)
-    widths = (wk, wk, wv, gates.shape[1])
-    return pl.pallas_call(
-        functools.partial(mix_kernel, n, segs, heads),
-        out_shape=(
-            jax.ShapeDtypeStruct((heads, n, BLOCK, HEAD_DIM), f32),
-            jax.ShapeDtypeStruct((heads, n, BLOCK, HEAD_DIM), bf16),
-            jax.ShapeDtypeStruct((heads, n, BLOCK, HEAD_DIM), bf16),
-            jax.ShapeDtypeStruct((heads, HEAD_DIM, 2 * HEAD_DIM), f32),
-            jax.ShapeDtypeStruct((n, rows, wv), bf16),
-        ),
-        in_specs=[pl.BlockSpec(memory_space=pltpu.SMEM)] + [anywhere] * 4 + [vmem],
-        out_specs=[vmem] * 5,
-        scratch_shapes=[pltpu.VMEM((n, half, w), bf16) for w in widths]
-        + [pltpu.VMEM((n, half, w), bf16) for w in widths]
-        + [
-            pltpu.VMEM((n, TAIL, 2 * wk + wv), bf16),
-            pltpu.VMEM((CONV, 2 * wk + wv), f32),
-            pltpu.VMEM((BLOCK + 8, 2 * wk + wv), f32),
-            pltpu.SemaphoreType.DMA((12, n)),
-            pltpu.SemaphoreType.DMA((12, n)),
-            pltpu.SemaphoreType.DMA((12,)),
-        ],
-        compiler_params=pltpu.CompilerParams(
-            collective_id=0, has_side_effects=True, vmem_limit_bytes=40 * 1024 * 1024
-        ),
-        name="mix",
-    )(order, qkv, z, gates, conv_weight, rates)
 
 
 def close_kernel(
@@ -346,16 +345,6 @@
     me = lax.axis_index("cp")
     final = segs - 1
     width = heads * HEAD_DIM
-    barrier = pltpu.get_barrier_semaphore()
-    for d in range(1, n):
-        pl.semaphore_signal(
-            barrier, inc=1, device_id=(seg, lax.rem(me + d, n)), device_id_type=MESH
-        )
-    pl.semaphore_signal(
-        barrier, inc=1, device_id=(lax.rem(seg + segs - 1, segs), me), device_id_type=MESH
-    )
-    pl.semaphore_wait(barrier, n)
-
     def hop(h):
         return pltpu.make_async_remote_copy(
             src_ref=pass_ref.at[h],
@@ -443,28 +432,65 @@
             hop(h).wait_send()
 
 
-def close(n, segs, heads, order, ends, o, mh, ml, z, gain):
+def whole_kernel(
+    n, segs, heads, order, qkv, z, gates, conv_weight, rate_ref, gain_ref, out,
+    o_ref, mh_ref, ml_ref, st_ref, oz, inc_ref, pass_ref, y_ref, *rest
+):
+    bufs, sems = rest[:11], rest[11:]
+    mix_kernel(
+        n, segs, heads, order, qkv, z, gates, conv_weight, rate_ref,
+        o_ref, mh_ref, ml_ref, st_ref, oz, *bufs, *sems[:3],
+    )
+    close_kernel(
+        n, segs, heads, order, st_ref, o_ref, mh_ref, ml_ref, oz, gain_ref, out,
+        inc_ref, pass_ref, y_ref, *sems[3:],
+    )
+
+
+def mixer(n, segs, heads, order, qkv, z, gates, conv_weight, rates, gain):
+    keys = max(1, heads // GROUP)
+    wk, wv = keys * HEAD_DIM, heads * HEAD_DIM
+    half = qkv.shape[0] // 2
+    anywhere = pl.BlockSpec(memory_space=pl.ANY)
     vmem = pl.BlockSpec(memory_space=pltpu.VMEM)
+    widths = (wk, wk, wv, gates.shape[1])
+    square = (HEAD_DIM, HEAD_DIM)
+    DMA = pltpu.SemaphoreType.DMA
     return pl.pallas_call(
-        functools.partial(close_kernel, n, segs, heads),
+        functools.partial(whole_kernel, n, segs, heads),
         out_shape=jax.ShapeDtypeStruct((BLOCK, n * heads * HEAD_DIM), bf16),
-        in_specs=[pl.BlockSpec(memory_space=pltpu.SMEM)] + [vmem] * 6,
+        in_specs=[pl.BlockSpec(memory_space=pltpu.SMEM)] + [anywhere] * 4 + [vmem] * 2,
         out_specs=vmem,
         scratch_shapes=[
-            pltpu.VMEM((heads, HEAD_DIM, HEAD_DIM), f32),
-            pltpu.VMEM((heads, HEAD_DIM, HEAD_DIM), f32),
+            pltpu.VMEM((heads, n, BLOCK, HEAD_DIM), f32),
             pltpu.VMEM((heads, n, BLOCK, HEAD_DIM), bf16),
-            pltpu.SemaphoreType.DMA((heads,)),
-            pltpu.SemaphoreType.DMA((heads,)),
-            pltpu.SemaphoreType.DMA((heads, n)),
-            pltpu.SemaphoreType.DMA((heads, n)),
-            pltpu.SemaphoreType.DMA((heads,)),
+            pltpu.VMEM((heads, n, BLOCK, HEAD_DIM), bf16),
+            pltpu.VMEM((heads, HEAD_DIM, 2 * HEAD_DIM), f32),
+            pltpu.VMEM((2 * n, half, wv), bf16),
+            pltpu.VMEM((heads,) + square, f32),
+            pltpu.VMEM((heads,) + square, f32),
+            pltpu.VMEM((heads, n, BLOCK, HEAD_DIM), bf16),
+        ]
+        + [pltpu.VMEM((n, half, w), bf16) for w in widths]
+        + [pltpu.VMEM((n, half, w), bf16) for w in widths]
+        + [
+            pltpu.VMEM((n, TAIL, 2 * wk + wv), bf16),
+            pltpu.VMEM((CONV, 2 * wk + wv), f32),
+            pltpu.VMEM((PAIR, BLOCK + 8, 2 * wk + wv), f32),
+            DMA((13, n)),
+            DMA((13, n)),
+            DMA((13,)),
+            DMA((heads,)),
+            DMA((heads,)),
+            DMA((heads, n)),
+            DMA((heads, n)),
+            DMA((heads,)),
         ],
         compiler_params=pltpu.CompilerParams(
-            collective_id=1, has_side_effects=True, vmem_limit_bytes=40 * 1024 * 1024
+            collective_id=0, has_side_effects=True, vmem_limit_bytes=56 * 1024 * 1024
         ),
-        name="close",
-    )(order, ends, o, mh, ml, z, gain)
+        name="mixer",
+    )(order, qkv, z, gates, conv_weight, rates, gain)
 
 
 def per_device(mixed_qkv, gate_z, gate_logits, block_table, conv_weight, a_log, dt_bias, norm_gain):
@@ -484,11 +510,9 @@
     rates = jnp.stack(
         [jnp.pad(-jnp.exp(a_log), (VALUE_HEADS, spare)), jnp.pad(dt_bias, (VALUE_HEADS, spare))]
     )
-    o, mh, ml, ends, z = mix(
-        n, segs, heads, order, mixed_qkv, gate_z, gate_logits, conv_weight, rates
+    return mixer(
+        n, segs, heads, order, mixed_qkv, gate_z, gate_logits, conv_weight, rates, norm_gain[None, :]
     )
-    z = z.reshape(blocks, z.shape[1] // 2, z.shape[2])
-    return close(n, segs, heads, order, ends, o, mh, ml, z, norm_gain[None, :])
 
 
 def solution(mesh):

time: 94.5 us -> 83.1 us (0.88)
  Pallas kernels: 81.8 us -> 70.9 us
  local copies, waits for them, and re-layouts: 6.25 us -> 4.45 us
  other arithmetic: 2.15 us -> 3.33 us
    pallas_call x2 -> x1, Pallas kernels: 81.8 us -> 70.9 us  [mixer(): pl.pallas_call(functools.partial(whole_kernel, n, segs, heads), out_shape...]
    unnamed x10 -> x2, local copies, waits for them, and re-layouts: 5.52 us -> 3.72 us
  transfers between devices with their start and end apart: 1 -> 1, of which waited for: 0 -> 0; matrix products, arithmetic and copies ran while one was open for 3% -> 5% of each run, Pallas kernels for 0% -> 0%
where the time goes in v2:
time: 83.1 us; the launch traced here: 82.8 us
  Pallas kernels  70.9 us (85%)
  local copies, waits for them, and re-layouts  4.45 us (5%)
  other arithmetic  3.33 us (4%)
  between operations  2.79 us (3%)
  starting transfers between devices  1.3 us (2%)
    pallas_call x1, Pallas kernels, mixer(): pl.pallas_call(functools.partial(whole_kernel, n, segs, heads), out_shape...  70.9 us
    unnamed x2, local copies, waits for them, and re-layouts  3.72 us
  transfers between devices with their start and end apart: 1, of which 0 were waited for; matrix products, arithmetic and copies ran while one was open for 5% of the time, Pallas kernels for 0%

profile of v2, /device:TPU:17, one launch (start us, length us, event | category | flops | bytes accessed | tf_op | source)
XLA Modules:
  0.0 82.8 jit_solution(14763027688582415390)
XLA Ops:
  0.0 1.3 %collective-permute-start = (s32[1,16]{1,0:T(1,128)}, s32[1,16]{1,0:T(1,128)S(1)}, u32[]{:S(2)}, u32[]{:S(2)}) collective-permute-start(s32[1,16]{1,0:T(1,128)} %param.11), channel_id=1, source_target_pairs={{0,8},{8,16},{16,24},{24,0},{1,9},{9,17},{17,25},{25,1},{2,10},{10... | collective-permute-start | bytes 200 | tf_op jit(solution)/shard_map/ppermute | solution.py:502
  1.3 0.7 exponential_negate_fusion
  2.0 0.8 select_reduce_fusion
  2.7 0.7 pad_bitcast_fusion
  3.5 0.6 pad_maximum_fusion.rate_ref
  4.1 1.4 %copy.10.gates = bf16[128,64]{1,0:T(8,128)(2,1)} copy(bf16[128,64]{0,1:T(8,128)(2,1)} %param.10) | data formatting | bytes 32768 | tf_op args[2]
  5.5 0.0 collective-permute-done
  5.5 0.7 fusion
  9.0 0.6 pad_add_fusion.order
  9.6 70.9 %mixer.1 = bf16[128,4096]{1,0:T(8,128)(2,1)} custom-call(s32[17]{0:T(128)} %pad_add_fusion.order, bf16[128,8192]{1,0:T(8,128)(2,1)} %qkv.1, bf16[128,4096]{1,0:T(8,128)(2,1)} %z.1, bf16[128,64]{1,0:T(8,128)(2,1)} %copy.10.gates, f32[4,8192]{1,0:T(4,128)} %conv_weight.1, f32[2,128]{1,0:T(2,128)} %pad_maximum_fusion.rate_ref, f32[1,128]{1,0:T(1,128)} %bitcast.11), custom_call_target="tpu_custom_call" | custom-call | tf_op jit(solution)/shard_map/mixer/pallas_call | solution.py:459
  80.5 2.3 %copy.12 = bf16[128,4096]{1,0:T(8,128)(2,1)} copy(bf16[128,4096]{1,0:T(8,128)(2,1)} %mixer.1) | data formatting | bytes 2097152
Async XLA Ops:
  0.0 5.5 %collective-permute-start = (s32[1,16]{1,0:T(1,128)}, s32[1,16]{1,0:T(1,128)S(1)}, u32[]{:S(2)}, u32[]{:S(2)}) collective-permute-start(s32[1,16]{1,0:T(1,128)} %param.11), channel_id=1, source_target_pairs={{0,8},{8,16},{16,24},{24,0},{1,9},{9,17},{17,25},{25,1},{2,10},{10... | collective-permute-start | bytes 200 | tf_op jit(solution)/shard_map/ppermute | solution.py:502
